TPU v7x, 32 devices: a whole 2x2x4 slice. The times are simulated.
32 devices in a mesh: region: 8 (over z, y), sub: 4 (over x, core).
Axes of the slice: x: 2, y: 2, z: 4, core: 2. Of those that a mesh axis runs over, the one named last changes fastest.
Arguments:
- density: bfloat16 [8, 4, 192, 2048], P('region', 'sub'), may hold values from -6 to 6
- inverse: bfloat16 [8, 4, 2048, 2048], P('region', 'sub'), may hold values from -0.125 to 0.125
- projection: bfloat16 [8, 4, 2048, 256], P('region', 'sub'), may hold values from -0.125 to 0.125
- points: float32 [8, 4, 3, 2048], P('region'), may hold values from 0 to 1
- skeleton_points: float32 [8, 4, 3, 256], replicated, may hold values from 0 to 1
- neighbours: int32 [8, 4, 2], P('region', 'sub'), may hold values from 0 to 3, as said below
- reads: int32 [8, 16, 2], replicated, may hold values from 0 to 7, as said below
Outputs:
- result: bfloat16 [8, 4, 192, 2048], P('region', 'sub')
Inputs may be any that keep to these rules, and one draw needn't show every extreme that they name: `neighbours`: each subdomain lists 2 distinct other subdomains of its own region. In reads[g], entries c * 4 to (c + 1) * 4 - 1 have block index // 2 equal to c; their owner regions are distinct and differ from g.
All inputs are finite; a program needn't handle non-finite values.
Results may differ from a plain program's by a relative error of at most 0.0067.
Values may be sent and summed in bfloat16 or wider, within the bound.
A program may use at most 128 MiB of HBM per device.

v0:
```python
import jax
import jax.numpy as jnp
from jax import lax
from jax.sharding import PartitionSpec as P

BLOCK_ROWS = 128


damping = 1.0
softening = 0.05


def kernel(source, target):
    apart_x = source[0][:, None] - target[0][None, :]
    apart_y = source[1][:, None] - target[1][None, :]
    apart_z = source[2][:, None] - target[2][None, :]
    squared = apart_x * apart_x + apart_y * apart_y + apart_z * apart_z
    kernel_tiles = jnp.exp(-damping * jnp.sqrt(squared)) / jnp.sqrt(squared + softening * softening)
    return (kernel_tiles * target.shape[1] ** (-0.5)).astype(jnp.bfloat16)


def per_device(density, inverse, projection, points, skeleton_points, neighbours, reads):
    sub_index = lax.axis_index("sub")
    region_index = lax.axis_index("region")
    groups = lax.axis_size("sub")
    local_rhs = density[0, 0]
    block_inverse = inverse[0, 0]
    rows_rhs = local_rhs.shape[0]
    solved = jnp.dot(local_rhs, block_inverse, preferred_element_type=jnp.float32).astype(
        jnp.bfloat16
    )
    strengths = jnp.dot(solved, projection[0, 0], preferred_element_type=jnp.float32).astype(
        jnp.bfloat16
    )
    region_points = points[0]
    own_points = lax.dynamic_index_in_dim(region_points, sub_index, 0, keepdims=False)
    listed = neighbours[0, 0]
    zeros_field = jnp.zeros(solved.shape, jnp.float32)
    shards = lax.all_gather(solved[None], "sub", axis=0, tiled=True)

    def add_one(offset, running):
        source = lax.dynamic_index_in_dim(shards, offset, 0, keepdims=False)
        mate_points = lax.dynamic_index_in_dim(region_points, offset, 0, keepdims=False)

        def evaluate(total):
            return total + jnp.dot(
                source, kernel(mate_points, own_points), preferred_element_type=jnp.float32
            )

        def unchanged(total):
            return total

        return lax.cond(jnp.any(listed == offset), evaluate, unchanged, running)

    near_field = lax.fori_loop(0, shards.shape[0], add_one, zeros_field)
    block_rows = BLOCK_ROWS
    blocks_each = strengths.shape[1] // block_rows
    per_column = reads.shape[1] // groups
    my_reads = lax.dynamic_index_in_dim(reads, region_index, 0, keepdims=False)
    column_reads = lax.dynamic_slice_in_dim(my_reads, sub_index * per_column, per_column, 0)
    owners = column_reads[:, 0]
    wanted = lax.dynamic_slice_in_dim(reads, sub_index * per_column, per_column, 1)
    matches = wanted[:, :, 0] == region_index
    present = jnp.any(matches, axis=1)
    halves = jnp.sum(jnp.where(matches, wanted[:, :, 1] % blocks_each, 0), axis=1)
    split_blocks = jnp.transpose(strengths.reshape(rows_rhs, blocks_each, block_rows), (1, 0, 2))
    outgoing = jnp.where(
        present[:, None, None], jnp.take(split_blocks, halves, axis=0), jnp.zeros((), jnp.bfloat16)
    )
    arrived = lax.all_to_all(outgoing, "region", split_axis=0, concat_axis=0, tiled=True)
    picked = jnp.take(arrived, owners, axis=0)
    add_shards = lax.all_gather(picked, "sub", axis=0, tiled=True)
    count_rows = add_shards.shape[0]
    group_size = 4

    def add_group(offset, running):
        first_row = offset * group_size
        entries = lax.dynamic_slice_in_dim(my_reads, first_row, group_size, 0)
        group_owners = entries[:, 0]
        group_columns = entries[:, 1] // blocks_each
        group_halves = entries[:, 1] % blocks_each
        located = skeleton_points[group_owners, group_columns].reshape(
            group_size, 3, blocks_each, block_rows
        )
        located = jnp.take_along_axis(located, group_halves[:, None, None, None], axis=2)[:, :, 0]
        sources = jnp.transpose(located, (1, 0, 2)).reshape(3, group_size * block_rows)
        values = lax.dynamic_slice_in_dim(add_shards, first_row, group_size, 0)
        values = jnp.transpose(values, (1, 0, 2)).reshape(rows_rhs, group_size * block_rows)
        return running + jnp.dot(
            values, kernel(sources, own_points), preferred_element_type=jnp.float32
        )

    far_field = lax.fori_loop(0, count_rows // group_size, add_group, zeros_field)
    applied = (local_rhs.astype(jnp.float32) + near_field + far_field).astype(jnp.bfloat16)
    result = jnp.dot(applied, block_inverse, preferred_element_type=jnp.float32).astype(
        jnp.bfloat16
    )
    return result[None, None]


def solution(mesh):
    return jax.shard_map(
        per_device,
        mesh=mesh,
        in_specs=(
            P("region", "sub", None, None),
            P("region", "sub", None, None),
            P("region", "sub", None, None),
            P("region", None, None, None),
            P(),
            P("region", "sub", None),
            P(),
        ),
        out_specs=P("region", "sub", None, None),
        check_vma=False,
    )
```

profile of v0, /device:TPU:0, one launch (start us, length us, event | category | flops | bytes accessed | tf_op | source)
XLA Modules:
  0.0 123.5 jit_solution(12675178542980507038)
XLA Ops:
  6.5 6.4 %fusion.33 = bf16[192,2048]{1,0:T(8,128)(2,1)} fusion(bf16[1,1,2048,2048]{3,2,1,0:T(8,128)(2,1)} %param.14, bf16[1,1,192,2048]{3,2,1,0:T(8,128)(2,1)} %param.13), kind=kOutput, calls=%fused_computation.63 | convolution fusion | flops 1611005952 | bytes 9961472 | tf_op jit(solution)/shard_map/dot_general | solution.py:29
  13.6 1.5 %fusion.42 = bf16[24,2,8,128]{3,2,1,0:T(8,128)(2,1)S(1)} fusion(bf16[192,2048]{1,0:T(8,128)(2,1)} %fusion.33, bf16[1,1,2048,256]{3,2,1,0:T(8,128)(2,1)S(1)} %copy-done), kind=kOutput, calls=%fused_computation.68 | convolution fusion | flops 201375744 | bytes 1933312 | tf_op jit(solution)/shard_map/dot_general | solution.py:32
  15.8 0.9 select_select_fusion
  16.7 7.3 %all-to-all-start = ((bf16[8,192,128]{2,1,0:T(8,128)(2,1)}), bf16[8,192,128]{2,1,0:T(8,128)(2,1)S(1)}, u32[]{:S(2)}, u32[]{:S(2)}) async-start(bf16[8,192,128]{2,1,0:T(8,128)(2,1)} %select_select_fusion), calls=%async_computation | async-start | bytes 786432 | tf_op jit(solution)/shard_map/all_to_all | solution.py:70
  25.6 10.1 %all-to-all-done = bf16[8,192,128]{2,1,0:T(8,128)(2,1)S(1)} async-done(((bf16[8,192,128]{2,1,0:T(8,128)(2,1)}), bf16[8,192,128]{2,1,0:T(8,128)(2,1)S(1)}, u32[]{:S(2)}, u32[]{:S(2)}) %all-to-all-start) | async-done | bytes 393248 | tf_op jit(solution)/shard_map/all_to_all | solution.py:70
  36.4 11.5 %all_gather.7 = bf16[16,192,128]{2,1,0:T(8,128)(2,1)S(1)} all-gather(bf16[4,192,128]{2,1,0:T(8,128)(2,1)S(1)} %broadcast_select_fusion), channel_id=1, replica_groups=mesh['region'=8,'sub'=4] {'sub'}, dimensions={0}, use_global_device_ids=true | all-gather | bytes 983040 | tf_op jit(solution)/shard_map/all_gather | solution.py:72
  47.9 24.9 %while.33 = (s32[]{:T(128)}, f32[192,2048]{1,0:T(8,128)S(1)}, bf16[16,192,128]{2,1,0:T(8,128)(2,1)S(1)}, s32[16,2]{0,1:T(2,128)S(1)}, f32[8,4,3,256]{3,2,1,0:T(4...) while((s32[]{:T(128)}, f32[192,2048]{1,0:T(8,128)S(1)}, ...), condition=%wide.region_8.9_spmd.clone, body=%wide.region_7.8_spmd.clone.sunk | while | flops 417072896 | bytes 4319797 | solution.py:93
  48.0 1.5 %gather_fusion = f32[4,3,256]{2,1,0:T(4,128)S(1)} fusion(f32[8,4,3,256]{3,2,1,0:T(4,128)} %get-tuple-element.545, s32[4]{0:T(128)S(1)} %get-tuple-element.513), kind=kCustom, calls=%fused_computation.clone.clone.1 | custom fusion | bytes 24608 | tf_op jit(solution)/shard_map/while/body/eval_jaxpr/gather | solution.py:82
  50.4 3.7 %convolution_add_fusion.2 = f32[192,2048]{1,0:T(8,128)S(1)} fusion(f32[2048]{0:T(1024)S(1)} %bitcast.130, f32[512]{0:T(512)S(1)} %bitcast.136, f32[2048]{0:T(1024)S(1)} %bitcast.131, f32[512]{0:T(512)S(1)} %bitcast.137, f32[2048]{0:T(1024)S(1)} %bitcast.129, f32[512]{0:T(512)S(1)} %bitcast.135, f32[192,2048]{1,0:T(8,128)S(1)} %get-tuple-element.532, ...), kind=kOutput, calls=%fused_computation.18.clone.1 | convolution fusion | flops 417071104 | bytes 3373057 | tf_op jit(solution)/shard_map/while/body/eval_jaxpr/dot_general | solution.py:89
  54.3 1.5 %gather_fusion = f32[4,3,256]{2,1,0:T(4,128)S(1)} fusion(f32[8,4,3,256]{3,2,1,0:T(4,128)} %get-tuple-element.545, s32[4]{0:T(128)S(1)} %get-tuple-element.513), kind=kCustom, calls=%fused_computation.clone.clone.1 | custom fusion | bytes 24608 | tf_op jit(solution)/shard_map/while/body/eval_jaxpr/gather | solution.py:82
  56.7 3.7 %convolution_add_fusion.2 = f32[192,2048]{1,0:T(8,128)S(1)} fusion(f32[2048]{0:T(1024)S(1)} %bitcast.130, f32[512]{0:T(512)S(1)} %bitcast.136, f32[2048]{0:T(1024)S(1)} %bitcast.131, f32[512]{0:T(512)S(1)} %bitcast.137, f32[2048]{0:T(1024)S(1)} %bitcast.129, f32[512]{0:T(512)S(1)} %bitcast.135, f32[192,2048]{1,0:T(8,128)S(1)} %get-tuple-element.532, ...), kind=kOutput, calls=%fused_computation.18.clone.1 | convolution fusion | flops 417071104 | bytes 3373057 | tf_op jit(solution)/shard_map/while/body/eval_jaxpr/dot_general | solution.py:89
  60.5 1.5 %gather_fusion = f32[4,3,256]{2,1,0:T(4,128)S(1)} fusion(f32[8,4,3,256]{3,2,1,0:T(4,128)} %get-tuple-element.545, s32[4]{0:T(128)S(1)} %get-tuple-element.513), kind=kCustom, calls=%fused_computation.clone.clone.1 | custom fusion | bytes 24608 | tf_op jit(solution)/shard_map/while/body/eval_jaxpr/gather | solution.py:82
  62.9 3.7 %convolution_add_fusion.2 = f32[192,2048]{1,0:T(8,128)S(1)} fusion(f32[2048]{0:T(1024)S(1)} %bitcast.130, f32[512]{0:T(512)S(1)} %bitcast.136, f32[2048]{0:T(1024)S(1)} %bitcast.131, f32[512]{0:T(512)S(1)} %bitcast.137, f32[2048]{0:T(1024)S(1)} %bitcast.129, f32[512]{0:T(512)S(1)} %bitcast.135, f32[192,2048]{1,0:T(8,128)S(1)} %get-tuple-element.532, ...), kind=kOutput, calls=%fused_computation.18.clone.1 | convolution fusion | flops 417071104 | bytes 3373057 | tf_op jit(solution)/shard_map/while/body/eval_jaxpr/dot_general | solution.py:89
  66.8 1.5 %gather_fusion = f32[4,3,256]{2,1,0:T(4,128)S(1)} fusion(f32[8,4,3,256]{3,2,1,0:T(4,128)} %get-tuple-element.545, s32[4]{0:T(128)S(1)} %get-tuple-element.513), kind=kCustom, calls=%fused_computation.clone.clone.1 | custom fusion | bytes 24608 | tf_op jit(solution)/shard_map/while/body/eval_jaxpr/gather | solution.py:82
  69.2 3.7 %convolution_add_fusion.2 = f32[192,2048]{1,0:T(8,128)S(1)} fusion(f32[2048]{0:T(1024)S(1)} %bitcast.130, f32[512]{0:T(512)S(1)} %bitcast.136, f32[2048]{0:T(1024)S(1)} %bitcast.131, f32[512]{0:T(512)S(1)} %bitcast.137, f32[2048]{0:T(1024)S(1)} %bitcast.129, f32[512]{0:T(512)S(1)} %bitcast.135, f32[192,2048]{1,0:T(8,128)S(1)} %get-tuple-element.532, ...), kind=kOutput, calls=%fused_computation.18.clone.1 | convolution fusion | flops 417071104 | bytes 3373057 | tf_op jit(solution)/shard_map/while/body/eval_jaxpr/dot_general | solution.py:89
  72.9 1.1 copy-done.1
  74.2 35.9 %while.32 = (s32[]{:T(128)}, f32[192,2048]{1,0:T(8,128)S(1)}, s32[2]{0:T(128)S(1)}, bf16[4,192,2048]{2,1,0:T(8,128)(2,1)}, f32[4,3,2048]{2,1,0:T(4,128)}, /*index=5*/f32[3,2048]{1,0:T(4,128)S(1)}, s32[]{:T(128)}) while((s32[]{:T(128)}, f32[192,2048]{1,0:T(8,128)S(1)}, s32[2]{0:T(128)S(1)}, bf16[4,192,2048]{2,1,0:T(8,128)(2,1)}, ...), condition=%wide.region_4.5_spmd, body=%wide.region_0.4_spmd.sunk | while | flops 1665531904 | bytes 4080315 | solution.py:55
  77.0 15.2 %conditional.2 = (f32[192,2048]{1,0:T(8,128)S(1)}) conditional(s32[]{:T(128)} %convert_element_type.63, f32[192,2048]{1,0:T(8,128)S(1)} %get-tuple-element.559, (s32[]{:T(128)}, bf16[4,192,2048]{2,1,0:T(8,128)(2,1)}, f32[4,3,2048]{2,1,0:T(4,128)}, f32[3,2048]{1,0:T(4,128)S(1)}, f32[192,2048]{1,0:T(8,128)S(1)}) %tuple.98), branch_computations={%region_2.2_spmd, %region_3.3_spmd} | conditional | flops 1665531904 | bytes 4080172 | solution.py:53
  77.0 0.9 constant_dynamic-slice_fusion.1
  77.9 14.3 %fusion.1 = f32[192,2048]{1,0:T(8,128)S(1)} fusion(f32[192,2048]{1,0:T(8,128)S(1)} %get-tuple-element.323, f32[2048]{0:T(1024)S(1)} %bitcast.133, f32[2048]{0:T(1024)S(1)} %bitcast.128, f32[2048]{0:T(1024)S(1)} %bitcast.134, f32[2048]{0:T(1024)S(1)} %bitcast.127, f32[2048]{0:T(1024)S(1)} %bitcast.132, f32[2048]{0:T(1024)S(1)} %bitcast.126, ...), kind=kOutput, calls=%fused_computation.6 | convolution fusion | flops 1665531904 | bytes 3981824 | tf_op jit(solution)/shard_map/while/body/eval_jaxpr/cond/branch_1_fun/dot_general | solution.py:46
  93.5 15.2 %conditional.2 = (f32[192,2048]{1,0:T(8,128)S(1)}) conditional(s32[]{:T(128)} %convert_element_type.63, f32[192,2048]{1,0:T(8,128)S(1)} %get-tuple-element.559, (s32[]{:T(128)}, bf16[4,192,2048]{2,1,0:T(8,128)(2,1)}, f32[4,3,2048]{2,1,0:T(4,128)}, f32[3,2048]{1,0:T(4,128)S(1)}, f32[192,2048]{1,0:T(8,128)S(1)}) %tuple.98), branch_computations={%region_2.2_spmd, %region_3.3_spmd} | conditional | flops 1665531904 | bytes 4080172 | solution.py:53
  93.5 0.9 constant_dynamic-slice_fusion.1
  94.5 14.3 %fusion.1 = f32[192,2048]{1,0:T(8,128)S(1)} fusion(f32[192,2048]{1,0:T(8,128)S(1)} %get-tuple-element.323, f32[2048]{0:T(1024)S(1)} %bitcast.133, f32[2048]{0:T(1024)S(1)} %bitcast.128, f32[2048]{0:T(1024)S(1)} %bitcast.134, f32[2048]{0:T(1024)S(1)} %bitcast.127, f32[2048]{0:T(1024)S(1)} %bitcast.132, f32[2048]{0:T(1024)S(1)} %bitcast.126, ...), kind=kOutput, calls=%fused_computation.6 | convolution fusion | flops 1665531904 | bytes 3981824 | tf_op jit(solution)/shard_map/while/body/eval_jaxpr/cond/branch_1_fun/dot_general | solution.py:46
  110.1 6.6 %fusion.39 = bf16[1,1,192,2048]{3,2,1,0:T(8,128)(2,1)} fusion(bf16[1,1,2048,2048]{3,2,1,0:T(8,128)(2,1)} %param.14, f32[192,2048]{1,0:T(8,128)} %copy-done.1, f32[192,2048]{1,0:T(8,128)S(1)} %get-tuple-element.344, bf16[1,1,192,2048]{3,2,1,0:T(8,128)(2,1)S(1)} %copy-done.2), kind=kOutput, calls=%fused_computation.65 | convolution fusion | flops 1612578816 | bytes 13107200 | tf_op jit(solution)/shard_map/dot_general | solution.py:95
  (103 shorter events, 10.5 us)
Async XLA Ops:
  6.5 7.1 %copy-start = (bf16[1,1,2048,256]{3,2,1,0:T(8,128)(2,1)S(1)}, bf16[1,1,2048,256]{3,2,1,0:T(8,128)(2,1)}, u32[]{:S(2)}) copy-start(bf16[1,1,2048,256]{3,2,1,0:T(8,128)(2,1)} %param.15) | copy-start | bytes 3145732
  6.5 6.4 %copy-start.5 = (s32[8,16,2]{1,2,0:T(2,128)S(1)}, s32[8,16,2]{1,2,0:T(2,128)}, u32[]{:S(2)}) copy-start(s32[8,16,2]{1,2,0:T(2,128)} %param.19) | copy-start | bytes 3076
  6.5 66.3 %all-gather.3.cloned.1.call-start = ((), (), s32[]{:S(2)}) async-start(), calls=%async_computation.1 | async-start | bytes 3932160 | tf_op jit(solution)/shard_map/all_gather | solution.py:39
  12.9 11.1 %copy-start.3 = (f32[1,4,3,2048]{3,1,2,0:T(4,128)S(1)}, f32[1,4,3,2048]{3,1,2,0:T(4,128)}, u32[]{:S(2)}) copy-start(f32[1,4,3,2048]{3,1,2,0:T(4,128)} %param.16) | copy-start | bytes 294916
  12.9 11.9 %copy-start.4 = (f32[8,4,3,256]{3,1,2,0:T(4,128)S(1)}, f32[8,4,3,256]{3,1,2,0:T(4,128)}, u32[]{:S(2)}) copy-start(f32[8,4,3,256]{3,1,2,0:T(4,128)} %param.17) | copy-start | bytes 294916
  16.7 19.0 %all-to-all-start = ((bf16[8,192,128]{2,1,0:T(8,128)(2,1)}), bf16[8,192,128]{2,1,0:T(8,128)(2,1)S(1)}, u32[]{:S(2)}, u32[]{:S(2)}) async-start(bf16[8,192,128]{2,1,0:T(8,128)(2,1)} %select_select_fusion), calls=%async_computation | async-start | bytes 786432 | tf_op jit(solution)/shard_map/all_to_all | solution.py:70
  47.9 26.3 %copy-start.6 = (s32[1,1,2]{2,1,0:T(1,128)S(1)}, s32[1,1,2]{2,1,0:T(1,128)}, u32[]{:S(2)}) copy-start(s32[1,1,2]{2,1,0:T(1,128)} %param.18) | copy-start | bytes 28
  72.8 1.2 copy-start.1
  74.2 35.9 %copy-start.2 = (bf16[1,1,192,2048]{3,2,1,0:T(8,128)(2,1)S(1)}, bf16[1,1,192,2048]{3,2,1,0:T(8,128)(2,1)}, u32[]{:S(2)}) copy-start(bf16[1,1,192,2048]{3,2,1,0:T(8,128)(2,1)} %param.13) | copy-start | bytes 2359300
Sparse Core Ops, SparseCore 0:
  13.1 34.1 all-gather.2
where the time goes:
time: 124 us
  matrix products  57.7 us (47%)
  local copies, waits for them, and re-layouts  15.6 us (13%)
  between operations  13.6 us (11%)
  blocking collectives  11.5 us (9%)
  waiting for transfers between devices  10.1 us (8%)
  starting transfers between devices  7.31 us (6%)
  other arithmetic  4.52 us (4%)
  loops' own time  3.2 us (3%)
    dot_general x2, matrix products, evaluate(): jnp.dot(source, kernel(mate_points, own_points), preferred_element_type=j...  28.5 us
    dot_general x4, matrix products, add_group(): jnp.dot(values, kernel(sources, own_points), preferred_element_type=jnp.f...  14.7 us
    all_gather x1, blocking collectives, per_device(): add_shards = lax.all_gather(picked, 'sub', axis=0, tiled=True)  11.5 us
    all_to_all x1, waiting for transfers between devices, per_device(): lax.all_to_all(outgoing, 'region', split_axis=0, concat_axis=0, tiled=True)  10.1 us
    all_to_all x1, starting transfers between devices, per_device(): lax.all_to_all(outgoing, 'region', split_axis=0, concat_axis=0, tiled=True)  7.31 us
    dot_general x1, matrix products, per_device(): jnp.dot(applied, block_inverse, preferred_element_type=jnp.float32)  6.56 us
    dot_general x1, matrix products, per_device(): jnp.dot(local_rhs, block_inverse, preferred_element_type=jnp.float32)  6.4 us
    gather x8, local copies, waits for them, and re-layouts, add_group(): skeleton_points[group_owners, group_columns]  5.96 us
  transfers between devices with their start and end apart: 2, of which 1 were waited for; matrix products, arithmetic and copies ran while one was open for 25% of the time, Pallas kernels for 0%

commit v1 on v0

v1 whole, which is shorter than its diff:
```python
import functools

import jax
import jax.numpy as jnp
from jax import lax
from jax.experimental import pallas as pl
from jax.experimental.pallas import tpu as pltpu
from jax.sharding import PartitionSpec as P

BLOCK_ROWS = 128
DAMPING = 1.0
SOFTENING = 0.05
LOG2E = 1.4426950408889634
FACTOR = DAMPING * LOG2E
FLOOR = 1e-30
TERMS = 24
ROWS = 256
PIECES = 4
MESH = pl.DeviceIdType.MESH
f32, bf16 = jnp.float32, jnp.bfloat16


def split(x):
    a = x.astype(bf16).astype(f32)
    b = (x - a).astype(bf16).astype(f32)
    c = (x - a - b).astype(bf16).astype(f32)
    return a, b, c


def prepared(coords):
    u = (coords - 0.5) * FACTOR
    norm = jnp.sum(u * u, axis=0, keepdims=True)
    return split(u), split(norm)


def fill_source(dst, coords, start):
    (a, b, c), (k, l, m) = prepared(coords)
    cols = pl.ds(start, coords.shape[1])
    for i, part in enumerate((a, a, b, b, a, c)):
        dst[3 * i : 3 * i + 3, cols] = part
    dst[18:19, cols] = k
    dst[19:20, cols] = l
    dst[20:21, cols] = m
    dst[21:24, cols] = jnp.ones((3, coords.shape[1]), f32)


def fill_target(dst, coords):
    (a, b, c), (k, l, m) = prepared(coords)
    for i, part in enumerate((a, b, a, b, c, a)):
        dst[3 * i : 3 * i + 3, :] = -2.0 * part
    dst[18:21, :] = jnp.ones((3, coords.shape[1]), f32)
    dst[21:22, :] = k
    dst[22:23, :] = l
    dst[23:24, :] = m


def body(n, regions, per_column, blocks_each,
         neighbours, reads, density, inverse, projection, points, skeleton,
         out,
         inv, near_k, far_k, shards, picked, arrived, outgoing, strengths, applied, total,
         source, target, far_source,
         inv_sem, x_send, x_recv, d_send, d_recv, f_send, f_recv,
         a_send, a_recv, px_send, px_recv, pd_send, pd_recv, pf_send, pf_recv):
    sub = lax.axis_index("sub")
    region = lax.axis_index("region")
    order = inv.shape[0]
    width = order // PIECES
    half = n // 2
    peer = sub + 1 - 2 * lax.rem(sub, 2)

    for p in range(PIECES):
        cols = pl.ds(p * width, width)
        pltpu.make_async_copy(inverse.at[0, 0, :, cols], inv.at[:, cols], inv_sem.at[p]).start()

    barrier = pltpu.get_barrier_semaphore()
    for k in range(1, n):
        pl.semaphore_signal(barrier, inc=1, device_id={"sub": lax.rem(sub + k, n)}, device_id_type=MESH)
    for k in range(1, regions):
        pl.semaphore_signal(barrier, inc=1, device_id={"region": lax.rem(region + k, regions)}, device_id_type=MESH)

    def remote(ref, dev, send, recv):
        return pltpu.make_async_remote_copy(
            src_ref=ref, dst_ref=ref, send_sem=send, recv_sem=recv, device_id=dev, device_id_type=MESH
        )

    def same(k):
        return lax.rem(sub + 2 * k, n)

    def origin(who, k):
        return lax.rem(who - 2 * k + n, n)

    def piece(o, p):
        return shards.at[o, :, pl.ds(p * width, width)]

    fill_target(target, points[0, sub])

    def send_piece(p):
        for k in range(1, half):
            remote(piece(sub, p), {"sub": same(k)}, x_send.at[k, p], x_recv.at[k, p]).start()
        remote(piece(sub, p), {"sub": peer}, d_send.at[p], d_recv.at[p]).start()

    for p in range(PIECES):
        cols = pl.ds(p * width, width)
        pltpu.make_async_copy(inverse.at[0, 0, :, cols], inv.at[:, cols], inv_sem.at[p]).wait()
        shards[sub, :, cols] = jnp.dot(
            density[0, 0], inv[:, cols], preferred_element_type=f32
        ).astype(bf16)
        if p == 0:
            pl.semaphore_wait(barrier, n - 1 + regions - 1)
        else:
            send_piece(p - 1)
    strengths[...] = jnp.dot(shards[sub], projection[0, 0], preferred_element_type=f32).astype(bf16)
    send_piece(PIECES - 1)

    def wanted(r):
        which = jnp.int32(0)
        for j in range(per_column):
            at = (r * per_column * n + sub * per_column + j) * 2
            which = which + jnp.where(reads[at] == region, lax.rem(reads[at + 1], blocks_each), 0)
        return which

    def pick_half(value, which):
        chosen = value[:, :BLOCK_ROWS]
        for b in range(1, blocks_each):
            chosen = jnp.where(which == b, value[:, b * BLOCK_ROWS : (b + 1) * BLOCK_ROWS], chosen)
        return chosen

    def exchange(k):
        return pltpu.make_async_remote_copy(
            src_ref=outgoing.at[k - 1], dst_ref=arrived.at[k - 1],
            send_sem=a_send.at[k], recv_sem=a_recv.at[k],
            device_id={"region": lax.rem(region + k, regions)}, device_id_type=MESH,
        )

    def prepare_out(k, _):
        outgoing[k - 1] = pick_half(strengths[...], wanted(lax.rem(region + k, regions)))
        return 0

    lax.fori_loop(1, regions, prepare_out, 0)

    def start_out(k, _):
        exchange(k).start()
        return 0

    lax.fori_loop(1, regions, start_out, 0)

    def generate(src, base, dst, rows):
        def step(i, _):
            at = pl.multiple_of(i * ROWS, ROWS)
            a = src[:, pl.ds(pl.multiple_of(base + at, ROWS), ROWS)].astype(bf16)
            for j in range(order // 256):
                b = target[:, j * 256 : (j + 1) * 256].astype(bf16)
                d2 = lax.dot_general(a, b, (((0,), (0,)), ((), ())), preferred_element_type=f32)
                d2 = jnp.maximum(d2.astype(bf16), jnp.array(FLOOR, bf16))
                decay = jnp.exp2(-(d2 * lax.rsqrt(d2)))
                soft = lax.rsqrt(d2 + jnp.array((FACTOR * SOFTENING) ** 2, bf16))
                dst[pl.ds(at, ROWS), j * 256 : (j + 1) * 256] = decay * soft
            return 0

        lax.fori_loop(0, rows // ROWS, step, 0)

    def forward(p):
        for k in range(1, half):
            o = origin(sub, k)
            remote(piece(o, p), {"sub": peer}, x_send.at[k, p], x_recv.at[k, p]).wait_recv()
            remote(piece(o, p), {"sub": peer}, f_send.at[k, p], f_recv.at[k, p]).start()

    mates = near_k.shape[0]
    p = 0
    for m in range(mates):
        fill_source(source, points[0, neighbours[m]], 0)
        generate(source, 0, near_k.at[m], order)
        if p < PIECES - 1:
            forward(p)
            p += 1

    def wait_out(k, _):
        exchange(k).wait_recv()
        return 0

    lax.fori_loop(1, regions, wait_out, 0)
    for j in range(per_column):
        at = ((region * n + sub) * per_column + j) * 2
        slot = jnp.maximum(lax.rem(region - reads[at] + regions, regions) - 1, 0)
        picked[sub, :, j * BLOCK_ROWS : (j + 1) * BLOCK_ROWS] = arrived[slot]

    far_w = per_column * BLOCK_ROWS
    for e in range(n * per_column):
        at = (region * n * per_column + e) * 2
        blk = reads[at + 1]
        located = skeleton[reads[at], lax.div(blk, blocks_each)]
        fill_source(far_source, pick_half(located, lax.rem(blk, blocks_each)), e * BLOCK_ROWS)

    for k in range(1, half):
        remote(picked.at[sub], {"sub": same(k)}, px_send.at[k], px_recv.at[k]).start()
    remote(picked.at[sub], {"sub": peer}, pd_send, pd_recv).start()

    ready = far_k.shape[0] // far_w
    generate(far_source, 0, far_k, far_k.shape[0])
    while p < PIECES:
        forward(p)
        p += 1
    for p in range(PIECES):
        remote(piece(peer, p), {"sub": peer}, d_send.at[p], d_recv.at[p]).wait_recv()
        for k in range(1, half):
            remote(piece(origin(peer, k), p), {"sub": peer}, f_send.at[k, p], f_recv.at[k, p]).wait_recv()

    tiles = order // width

    def near_tile(t, _):
        cols = pl.ds(pl.multiple_of(t * width, width), width)
        acc = jnp.dot(shards[neighbours[0]], near_k[0, :, cols], preferred_element_type=f32)
        for m in range(1, mates):
            acc += jnp.dot(shards[neighbours[m]], near_k[m, :, cols], preferred_element_type=f32)
        total[:, cols] = acc
        return 0

    lax.fori_loop(0, tiles, near_tile, 0)

    for k in range(1, half):
        o = origin(sub, k)
        remote(picked.at[o], {"sub": peer}, px_send.at[k], px_recv.at[k]).wait_recv()
        remote(picked.at[o], {"sub": peer}, pf_send.at[k], pf_recv.at[k]).start()
    remote(picked.at[peer], {"sub": peer}, pd_send, pd_recv).wait_recv()
    for k in range(1, half):
        remote(picked.at[origin(peer, k)], {"sub": peer}, pf_send.at[k], pf_recv.at[k]).wait_recv()

    for c in range(ready, n):
        generate(far_source, c * far_w, near_k.at[0], far_w)

        def more(t, _):
            cols = pl.ds(pl.multiple_of(t * width, width), width)
            total[:, cols] += jnp.dot(picked[c], near_k[0, :far_w, cols], preferred_element_type=f32)
            return 0

        lax.fori_loop(0, tiles, more, 0)

    scale = FACTOR * order ** -0.5

    def far_tile(t, _):
        cols = pl.ds(pl.multiple_of(t * width, width), width)
        acc = total[:, cols]
        for c in range(ready):
            acc += jnp.dot(
                picked[c], far_k[c * far_w : (c + 1) * far_w, cols], preferred_element_type=f32
            )
        applied[:, cols] = (density[0, 0, :, cols].astype(f32) + scale * acc).astype(bf16)
        return 0

    lax.fori_loop(0, tiles, far_tile, 0)

    def result_tile(t, _):
        cols = pl.ds(pl.multiple_of(t * width, width), width)
        out[0, 0, :, cols] = jnp.dot(
            applied[...], inv[:, cols], preferred_element_type=f32
        ).astype(bf16)
        return 0

    lax.fori_loop(0, tiles, result_tile, 0)

    def drain(k, _):
        exchange(k).wait_send()
        return 0

    lax.fori_loop(1, regions, drain, 0)
    for p in range(PIECES):
        remote(piece(sub, p), {"sub": peer}, d_send.at[p], d_recv.at[p]).wait_send()
        for k in range(1, half):
            remote(piece(sub, p), {"sub": same(k)}, x_send.at[k, p], x_recv.at[k, p]).wait_send()
            remote(piece(origin(sub, k), p), {"sub": peer}, f_send.at[k, p], f_recv.at[k, p]).wait_send()
    remote(picked.at[sub], {"sub": peer}, pd_send, pd_recv).wait_send()
    for k in range(1, half):
        remote(picked.at[sub], {"sub": same(k)}, px_send.at[k], px_recv.at[k]).wait_send()
        remote(picked.at[origin(sub, k)], {"sub": peer}, pf_send.at[k], pf_recv.at[k]).wait_send()


def per_device(density, inverse, projection, points, skeleton_points, neighbours, reads):
    n = lax.axis_size("sub")
    regions = lax.axis_size("region")
    _, _, rows, order = density.shape
    rank = projection.shape[3]
    blocks_each = rank // BLOCK_ROWS
    per_column = reads.shape[1] // n
    mates = neighbours.shape[2]
    far_w = per_column * BLOCK_ROWS
    ready = min(n, max(1, order // far_w))
    half = n // 2
    dma = pltpu.SemaphoreType.DMA
    vmem = pl.BlockSpec(memory_space=pltpu.VMEM)
    smem = pl.BlockSpec(memory_space=pltpu.SMEM)
    return pl.pallas_call(
        functools.partial(body, n, regions, per_column, blocks_each),
        out_shape=jax.ShapeDtypeStruct(density.shape, bf16),
        in_specs=[smem, smem, vmem, pl.BlockSpec(memory_space=pl.ANY), vmem, vmem, vmem],
        out_specs=vmem,
        scratch_shapes=[
            pltpu.VMEM((order, order), bf16),
            pltpu.VMEM((mates, order, order), bf16),
            pltpu.VMEM((ready * far_w, order), bf16),
            pltpu.VMEM((n, rows, order), bf16),
            pltpu.VMEM((n, rows, far_w), bf16),
            pltpu.VMEM((regions - 1, rows, BLOCK_ROWS), bf16),
            pltpu.VMEM((regions - 1, rows, BLOCK_ROWS), bf16),
            pltpu.VMEM((rows, rank), bf16),
            pltpu.VMEM((rows, order), bf16),
            pltpu.VMEM((rows, order), f32),
            pltpu.VMEM((TERMS, order), f32),
            pltpu.VMEM((TERMS, order), f32),
            pltpu.VMEM((TERMS, n * far_w), f32),
            dma((PIECES,)),
            dma((half, PIECES)), dma((half, PIECES)),
            dma((PIECES,)), dma((PIECES,)),
            dma((half, PIECES)), dma((half, PIECES)),
            dma((regions,)), dma((regions,)),
            dma((half,)), dma((half,)),
            dma, dma,
            dma((half,)), dma((half,)),
        ],
        compiler_params=pltpu.CompilerParams(
            collective_id=0, has_side_effects=True, vmem_limit_bytes=60 * 1024 * 1024
        ),
    )(neighbours.reshape(-1), reads.reshape(-1), density, inverse, projection, points, skeleton_points)


def solution(mesh):
    return jax.shard_map(
        per_device,
        mesh=mesh,
        in_specs=(
            P("region", "sub", None, None),
            P("region", "sub", None, None),
            P("region", "sub", None, None),
            P("region", None, None, None),
            P(),
            P("region", "sub", None),
            P(),
        ),
        out_specs=P("region", "sub", None, None),
        check_vma=False,
    )
```

time: 124 us -> 56.1 us (0.45)
  matrix products: 57.7 us -> 0 us
  Pallas kernels: 0 us -> 49 us
  between operations: 13.6 us -> 0.01 us
  blocking collectives: 11.5 us -> 0 us
  waiting for transfers between devices: 10.1 us -> 0 us
  local copies, waits for them, and re-layouts: 15.6 us -> 6.77 us
  starting transfers between devices: 7.31 us -> 0 us
  other arithmetic: 4.52 us -> 0 us
  loops' own time: 3.2 us -> 0 us
    dot_general x9 -> x0, matrix products: 57.7 us -> none  [the longest x2 28.5 us: evaluate(): jnp.dot(source, kernel(mate_points, own_points), preferred_element_type=j...]
    pallas_call x0 -> x1, Pallas kernels: none -> 49 us  [per_device(): pl.pallas_call(functools.partial(body, n, regions, per_column, blocks_eac...]
    all_gather x1 -> x0, blocking collectives: 11.5 us -> none  [per_device(): add_shards = lax.all_gather(picked, 'sub', axis=0, tiled=True)]
    all_to_all x1 -> x0, waiting for transfers between devices: 10.1 us -> none  [per_device(): lax.all_to_all(outgoing, 'region', split_axis=0, concat_axis=0, tiled=True)]
    gather x14 -> x0, local copies, waits for them, and re-layouts: 9.49 us -> none  [the longest x8 5.96 us: add_group(): skeleton_points[group_owners, group_columns]]
    all_to_all x1 -> x0, starting transfers between devices: 7.31 us -> none  [per_device(): lax.all_to_all(outgoing, 'region', split_axis=0, concat_axis=0, tiled=True)]
    unnamed x17 -> x4, local copies, waits for them, and re-layouts: 2.58 us -> 6.09 us
    another operation x6 -> x0, loops' own time: 3.2 us -> none  [the longest x1 2.83 us: per_device(): near_field = lax.fori_loop(0, shards.shape[0], add_one, zeros_field)]
  transfers between devices with their start and end apart: 2 -> 0, of which waited for: 1 -> 0; matrix products, arithmetic and copies ran while one was open for 25% -> 0% of each run, Pallas kernels for 0% -> 0%
where the time goes in v1:
time: 56.1 us; the launch traced here: 55.8 us
  Pallas kernels  49 us (87%)
  local copies, waits for them, and re-layouts  6.77 us (12%)
    pallas_call x1, Pallas kernels, per_device(): pl.pallas_call(functools.partial(body, n, regions, per_column, blocks_eac...  49 us
    unnamed x4, local copies, waits for them, and re-layouts  6.09 us

profile of v1, /device:TPU:0, one launch (start us, length us, event | category | flops | bytes accessed | tf_op | source)
XLA Modules:
  0.0 55.8 jit_solution(16171339160043524222)
XLA Ops:
  0.0 0.8 %copy.10 = s32[8,16,2]{2,1,0:T(8,128)S(1)} copy(s32[8,16,2]{1,2,0:T(2,128)} %param.13) | data formatting | bytes 2048 | tf_op args[6]
  0.8 0.7 %reshape.7.reads = s32[256]{0:T(256)} reshape(s32[8,16,2]{2,1,0:T(8,128)S(1)} %copy.10) | data formatting | bytes 2048 | tf_op jit(solution)/shard_map/reshape | solution.py:322
  1.5 1.6 %copy.11.points = f32[1,4,3,2048]{3,2,1,0:T(4,128)} copy(f32[1,4,3,2048]{3,1,2,0:T(4,128)} %param.10) | data formatting | bytes 196608 | tf_op args[3]
  3.1 1.6 %copy.12.skeleton = f32[8,4,3,256]{3,2,1,0:T(4,128)} copy(f32[8,4,3,256]{3,1,2,0:T(4,128)} %param.11) | data formatting | bytes 196608 | tf_op args[4]
  4.7 49.0 %shard_map.73 = bf16[1,1,192,2048]{3,2,1,0:T(8,128)(2,1)} custom-call(s32[2]{0:T(128)} %bitcast.1, s32[256]{0:T(256)} %reshape.7.reads, bf16[1,1,192,2048]{3,2,1,0:T(8,128)(2,1)} %density.1, bf16[1,1,2048,2048]{3,2,1,0:T(8,128)(2,1)} %inverse.1, bf16[1,1,2048,256]{3,2,1,0:T(8,128)(2,1)} %projection.1, f32[1,4,3,2048]{3,2,1,0:T(4,128)} %copy.11.points, ...), custom_call_target="tpu_custom_call" | custom-call | tf_op jit(solution)/shard_map/pallas_call | solution.py:291
  53.7 2.1 %copy.14 = bf16[1,1,192,2048]{3,2,1,0:T(8,128)(2,1)} copy(bf16[1,1,192,2048]{3,2,1,0:T(8,128)(2,1)} %shard_map.73) | data formatting | bytes 1572864
